TPU v7x, 32 devices: a whole 2x2x4 slice. The times are simulated.
32 devices in a mesh: dp: 4 (over z), ctx: 2 (over x), tp: 4 (over y, core).
Axes of the slice: x: 2, y: 2, z: 4, core: 2. Of those that a mesh axis runs over, the one named last changes fastest.
Arguments:
- tokens: bfloat16 [4096, 2048], P(('dp', 'ctx')), may hold values from -6 to 6
- segments: int32 [4, 1024], P('dp'), may hold values from 0 to 3, never falling along the last dimension, each value on 1 to 512 neighbouring positions
- attn_gain: float32 [2048], replicated, may hold values from 0.5 to 1.5
- query_weight: bfloat16 [2048, 2048], P(None, 'tp'), may hold values from -0.125 to 0.125
- key_weight: bfloat16 [2048, 256], P(None, 'tp'), may hold values from -0.125 to 0.125
- value_weight: bfloat16 [2048, 256], P(None, 'tp'), may hold values from -0.125 to 0.125
- output_weight: bfloat16 [2048, 2048], P('tp'), may hold values from -2 to 2
- mlp_gain: float32 [2048], replicated, may hold values from 0.5 to 1.5
- gate_weight: bfloat16 [2048, 5632], P(None, 'tp'), may hold values from -0.125 to 0.125
- up_weight: bfloat16 [2048, 5632], P(None, 'tp'), may hold values from -0.125 to 0.125
- down_weight: bfloat16 [5632, 2048], P('tp'), may hold values from -0.078125 to 0.078125
- cotangent: bfloat16 [4096, 2048], P(('dp', 'ctx')), may hold values from -6 to 6
Outputs:
- layer_out: float32 [4096, 2048], P(('dp', 'ctx'))
- tokens_grad: float32 [4096, 2048], P(('dp', 'ctx'))
- attn_gain_grad: float32 [2048], P(('dp', 'ctx'))
- query_grad: float32 [2048, 2048], P(('dp', 'ctx'), 'tp')
- key_grad: float32 [2048, 256], P(('dp', 'ctx'), 'tp')
- value_grad: float32 [2048, 256], P(('dp', 'ctx'), 'tp')
- output_grad: float32 [2048, 2048], P('tp', ('dp', 'ctx'))
- mlp_gain_grad: float32 [2048], P(('dp', 'ctx'))
- gate_grad: float32 [2048, 5632], P(('dp', 'ctx'), 'tp')
- up_grad: float32 [2048, 5632], P(('dp', 'ctx'), 'tp')
- down_grad: float32 [5632, 2048], P('tp', ('dp', 'ctx'))
Inputs may be any that keep to these rules, and one draw needn't show every extreme that they name: `segments`: along each packed sequence the document numbers never fall; a document has 1 to 512 tokens, and one document of each sequence has exactly 512.
All inputs are finite; a program needn't handle non-finite values.
Results may differ from a plain program's by a relative error of at most 0.013.
Values may be sent and summed in bfloat16 or wider, within the bound.
A program may use at most 192 MiB of HBM per device.

v0:
```python
import jax
import jax.numpy as jnp
from jax import lax
from jax.sharding import PartitionSpec as P

HEAD = 64
EPSILON = 1e-05
MASKED = -1000000000.0


def contract(left_side, right_side, left_dim, right_dim):
    return lax.dot_general(
        left_side,
        right_side,
        (((left_dim,), (right_dim,)), ((), ())),
        preferred_element_type=jnp.float32,
    )


def rms_parts(values, gain_vec):
    inverse = lax.rsqrt(jnp.mean(values * values, axis=-1, keepdims=True) + EPSILON)
    normed = values * inverse
    return (normed, inverse, (normed * gain_vec).astype(jnp.bfloat16))


def rms_back(grad_out, normed, inverse, gain_vec):
    scaled = grad_out * gain_vec
    input_back = inverse * (scaled - normed * jnp.mean(scaled * normed, axis=-1, keepdims=True))
    return (input_back, jnp.sum(grad_out * normed, axis=0))


def rope_tables(positions, head_width):
    frequency = 10000.0 ** (-jnp.arange(0, head_width, 2, dtype=jnp.float32) / head_width)
    angles = positions.astype(jnp.float32)[:, None] * frequency[None, :]
    cos_table = jnp.concatenate([jnp.cos(angles), jnp.cos(angles)], -1)
    sin_table = jnp.concatenate([jnp.sin(angles), jnp.sin(angles)], -1)
    return (cos_table, sin_table)


def rotate(values, cos_table, sin_table):
    half_width = values.shape[-1] // 2
    turned = jnp.concatenate([-values[..., half_width:], values[..., :half_width]], -1)
    return values * cos_table[:, None, :] + turned * sin_table[:, None, :]


def rotate_back(gradients, cos_table, sin_table):
    half_width = gradients.shape[-1] // 2
    scaled = gradients * sin_table[:, None, :]
    turned = jnp.concatenate([scaled[..., half_width:], -scaled[..., :half_width]], -1)
    return gradients * cos_table[:, None, :] + turned


def block_scores(queries, keys_blk, allowed, score_scale):
    raw_scores = (
        jnp.einsum("bgnd,kgd->gnbk", queries, keys_blk, preferred_element_type=jnp.float32)
        * score_scale
    )
    return jnp.where(allowed[None, None], raw_scores, MASKED)


def shards(
    tokens,
    segments,
    attn_gain,
    query_weight,
    key_weight,
    value_weight,
    output_weight,
    mlp_gain,
    gate_weight,
    up_weight,
    down_weight,
    cotangent,
):
    row_count = tokens.shape[0]
    kv_local = key_weight.shape[1] // HEAD
    q_local = query_weight.shape[1] // HEAD
    groups = q_local // kv_local
    kv_width = kv_local * HEAD
    score_scale = HEAD ** (-0.5)
    ctx_rank = lax.axis_index("ctx")
    ctx_count = lax.axis_size("ctx")
    offsets = jnp.arange(row_count, dtype=jnp.int32)
    query_pos = ctx_rank * row_count + offsets
    seq_segs = segments[0]
    seq_rows = seq_segs.shape[0]
    query_segs = lax.dynamic_slice_in_dim(seq_segs, ctx_rank * row_count, row_count)
    cos_table, sin_table = rope_tables(query_pos, HEAD)
    tokens_wide = tokens.astype(jnp.float32)
    normed_one, inverse_one, attn_in = rms_parts(tokens_wide, attn_gain)
    queries = contract(attn_in, query_weight, 1, 0).reshape(row_count, q_local, HEAD)
    keys_pre = contract(attn_in, key_weight, 1, 0).reshape(row_count, kv_local, HEAD)
    values_pre = contract(attn_in, value_weight, 1, 0)
    queries_rot = (
        rotate(queries, cos_table, sin_table)
        .astype(jnp.bfloat16)
        .reshape(row_count, kv_local, groups, HEAD)
    )
    keys_rot = (
        rotate(keys_pre, cos_table, sin_table).astype(jnp.bfloat16).reshape(row_count, kv_width)
    )
    local_kv = jnp.concatenate([keys_rot, values_pre.astype(jnp.bfloat16)], axis=1)
    whole_kv = lax.all_gather(local_kv, "ctx", axis=0, tiled=True)

    def key_block(kv_rows_all, block_index):
        first_row = block_index * row_count
        kv_piece = lax.dynamic_slice_in_dim(kv_rows_all, first_row, row_count, 0)
        key_segs = lax.dynamic_slice_in_dim(seq_segs, first_row, row_count)
        allowed = (query_segs[:, None] == key_segs[None, :]) & (
            (first_row + offsets)[None, :] <= query_pos[:, None]
        )
        keys_blk = kv_piece[:, :kv_width].reshape(row_count, kv_local, HEAD)
        values_blk = kv_piece[:, kv_width:].reshape(row_count, kv_local, HEAD)
        return (keys_blk, values_blk, allowed)

    def max_step(block_index, state_pair):
        running_max, running_sum = state_pair
        keys_blk, values_blk, allowed = key_block(whole_kv, block_index)
        scores = block_scores(queries_rot, keys_blk, allowed, score_scale)
        new_max = jnp.maximum(running_max, jnp.max(scores, axis=-1))
        new_sum = running_sum * jnp.exp(running_max - new_max) + jnp.sum(
            jnp.exp(scores - new_max[..., None]), axis=-1
        )
        return (new_max, new_sum)

    start_max = jnp.full((kv_local, groups, row_count), MASKED, jnp.float32)
    row_max, row_sum = lax.fori_loop(0, ctx_count, max_step, (start_max, jnp.zeros_like(start_max)))
    log_total = row_max + jnp.log(row_sum)

    def out_step(block_index, mixed_heads):
        keys_blk, values_blk, allowed = key_block(whole_kv, block_index)
        soft_weights = jnp.exp(
            block_scores(queries_rot, keys_blk, allowed, score_scale) - log_total[..., None]
        ).astype(jnp.bfloat16)
        return mixed_heads + jnp.einsum(
            "gnbk,kgd->bgnd", soft_weights, values_blk, preferred_element_type=jnp.float32
        )

    mixed_heads = lax.fori_loop(
        0, ctx_count, out_step, jnp.zeros((row_count, kv_local, groups, HEAD), jnp.float32)
    )
    heads_out = mixed_heads.reshape(row_count, q_local * HEAD).astype(jnp.bfloat16)
    branch = lax.psum(contract(heads_out, output_weight, 1, 0), "tp")
    middle = tokens_wide + branch
    normed_two, inverse_two, mlp_in = rms_parts(middle, mlp_gain)
    gate_pre = contract(mlp_in, gate_weight, 1, 0)
    up_pre = contract(mlp_in, up_weight, 1, 0)
    sigmoid_gate = jax.nn.sigmoid(gate_pre)
    silu_gate = gate_pre * sigmoid_gate
    hidden = (silu_gate * up_pre).astype(jnp.bfloat16)
    layer_out = middle + lax.psum(
        contract(hidden, down_weight, 1, 0).astype(jnp.bfloat16), "tp"
    ).astype(jnp.float32)
    cot_wide = cotangent.astype(jnp.float32)
    down_grad = contract(hidden, cotangent, 0, 0)
    hidden_back = contract(cotangent, down_weight, 1, 1)
    gate_back = (
        hidden_back * up_pre * sigmoid_gate * (1.0 + gate_pre * (1.0 - sigmoid_gate))
    ).astype(jnp.bfloat16)
    up_back = (hidden_back * silu_gate).astype(jnp.bfloat16)
    gate_grad = contract(mlp_in, gate_back, 0, 0)
    up_grad = contract(mlp_in, up_back, 0, 0)
    mlp_in_back = lax.psum(
        contract(gate_back, gate_weight, 1, 1) + contract(up_back, up_weight, 1, 1), "tp"
    )
    middle_part, mlp_gain_grad = rms_back(mlp_in_back, normed_two, inverse_two, mlp_gain)
    middle_back = cot_wide + middle_part
    mlp_done = (gate_grad, up_grad, down_grad, mlp_gain_grad)
    branch_back = middle_back.astype(jnp.bfloat16)
    output_grad = contract(heads_out, branch_back, 0, 0)
    heads_back = (
        contract(branch_back, output_weight, 1, 1)
        .astype(jnp.bfloat16)
        .reshape(row_count, kv_local, groups, HEAD)
    )

    def delta_step(block_index, delta_rows):
        keys_blk, values_blk, allowed = key_block(whole_kv, block_index)
        soft_weights = jnp.exp(
            block_scores(queries_rot, keys_blk, allowed, score_scale) - log_total[..., None]
        )
        weight_back = jnp.einsum(
            "bgnd,kgd->gnbk", heads_back, values_blk, preferred_element_type=jnp.float32
        )
        return delta_rows + jnp.sum(soft_weights * weight_back, axis=-1)

    delta_rows = lax.fori_loop(
        0, ctx_count, delta_step, jnp.zeros((kv_local, groups, row_count), jnp.float32)
    )

    def grad_step(block_index, state_pair):
        query_acc, kv_acc = state_pair
        keys_blk, values_blk, allowed = key_block(whole_kv, block_index)
        soft_weights = jnp.exp(
            block_scores(queries_rot, keys_blk, allowed, score_scale) - log_total[..., None]
        )
        weight_back = jnp.einsum(
            "bgnd,kgd->gnbk", heads_back, values_blk, preferred_element_type=jnp.float32
        )
        score_back = (soft_weights * (weight_back - delta_rows[..., None])).astype(jnp.bfloat16)
        query_acc = (
            query_acc
            + jnp.einsum("gnbk,kgd->bgnd", score_back, keys_blk, preferred_element_type=jnp.float32)
            * score_scale
        )
        key_part = (
            jnp.einsum(
                "gnbk,bgnd->kgd", score_back, queries_rot, preferred_element_type=jnp.float32
            )
            * score_scale
        )
        value_part = jnp.einsum(
            "gnbk,bgnd->kgd",
            soft_weights.astype(jnp.bfloat16),
            heads_back,
            preferred_element_type=jnp.float32,
        )
        both_parts = jnp.concatenate(
            [key_part.reshape(row_count, kv_width), value_part.reshape(row_count, kv_width)], axis=1
        )
        first_row = block_index * row_count
        updated = lax.dynamic_slice_in_dim(kv_acc, first_row, row_count, 0) + both_parts
        kv_acc = lax.dynamic_update_slice_in_dim(kv_acc, updated, first_row, 0)
        return (query_acc, kv_acc)

    start_query = jnp.zeros((row_count, kv_local, groups, HEAD), jnp.float32)
    start_kv = jnp.zeros((seq_rows, 2 * kv_width), jnp.float32)
    query_acc, kv_acc = lax.fori_loop(0, ctx_count, grad_step, (start_query, start_kv))
    kv_grad = lax.psum_scatter(kv_acc, "ctx", scatter_dimension=0, tiled=True)
    key_back = (
        rotate_back(kv_grad[:, :kv_width].reshape(row_count, kv_local, HEAD), cos_table, sin_table)
        .reshape(row_count, kv_width)
        .astype(jnp.bfloat16)
    )
    value_back = kv_grad[:, kv_width:].astype(jnp.bfloat16)
    query_back = (
        rotate_back(query_acc.reshape(row_count, q_local, HEAD), cos_table, sin_table)
        .reshape(row_count, q_local * HEAD)
        .astype(jnp.bfloat16)
    )
    query_grad = contract(attn_in, query_back, 0, 0)
    key_grad = contract(attn_in, key_back, 0, 0)
    value_grad = contract(attn_in, value_back, 0, 0)
    attn_in_back = lax.psum(
        contract(query_back, query_weight, 1, 1)
        + contract(key_back, key_weight, 1, 1)
        + contract(value_back, value_weight, 1, 1),
        "tp",
    )
    tokens_part, attn_gain_grad = rms_back(attn_in_back, normed_one, inverse_one, attn_gain)
    tokens_grad = middle_back + tokens_part
    finals = (
        lax.psum_scatter(attn_gain_grad, ("dp", "ctx"), scatter_dimension=0, tiled=True),
        lax.psum_scatter(query_grad, ("dp", "ctx"), scatter_dimension=0, tiled=True),
        lax.psum_scatter(key_grad, ("dp", "ctx"), scatter_dimension=0, tiled=True),
        lax.psum_scatter(value_grad, ("dp", "ctx"), scatter_dimension=0, tiled=True),
        lax.psum_scatter(output_grad, ("dp", "ctx"), scatter_dimension=1, tiled=True),
        lax.psum_scatter(mlp_done[3], ("dp", "ctx"), scatter_dimension=0, tiled=True),
        lax.psum_scatter(mlp_done[0], ("dp", "ctx"), scatter_dimension=0, tiled=True),
        lax.psum_scatter(mlp_done[1], ("dp", "ctx"), scatter_dimension=0, tiled=True),
        lax.psum_scatter(mlp_done[2], ("dp", "ctx"), scatter_dimension=1, tiled=True),
    )
    return (
        layer_out,
        tokens_grad,
        finals[0],
        finals[1],
        finals[2],
        finals[3],
        finals[4],
        finals[5],
        finals[6],
        finals[7],
        finals[8],
    )


def solution(mesh):
    return jax.shard_map(
        shards,
        mesh=mesh,
        in_specs=(
            P(("dp", "ctx"), None),
            P("dp", None),
            P(),
            P(None, "tp"),
            P(None, "tp"),
            P(None, "tp"),
            P("tp", None),
            P(),
            P(None, "tp"),
            P(None, "tp"),
            P("tp", None),
            P(("dp", "ctx"), None),
        ),
        out_specs=(
            P(("dp", "ctx"), None),
            P(("dp", "ctx"), None),
            P(("dp", "ctx")),
            P(("dp", "ctx"), "tp"),
            P(("dp", "ctx"), "tp"),
            P(("dp", "ctx"), "tp"),
            P("tp", ("dp", "ctx")),
            P(("dp", "ctx")),
            P(("dp", "ctx"), "tp"),
            P(("dp", "ctx"), "tp"),
            P("tp", ("dp", "ctx")),
        ),
        check_vma=False,
    )
```

profile of v0, /device:TPU:0, one launch (start us, length us, event | category | flops | bytes accessed | tf_op | source)
XLA Modules:
  0.0 1377.9 jit_solution(10986597939069724232)
XLA Ops:
  14.9 7.3 all_gather.3
  27.9 11.2 while.60
  39.8 12.4 while.61
  57.0 86.9 %all-reduce.8.cloned.1.call-done = f32[512,2048]{1,0:T(8,128)} async-done(((f32[512,2048]{1,0:T(8,128)}), f32[512,2048]{1,0:T(8,128)}) %all-reduce.8.cloned.1.call-update) | async-done | bytes 4194320 | tf_op jit(solution)/shard_map/psum | solution.py:143
  147.9 10.0 fusion.104
  163.0 8.0 multiply_convert_fusion.1
  181.1 7.8 convolution_convert_fusion
  189.4 77.4 %all-reduce.12.cloned.1.call-done = f32[512,2048]{1,0:T(8,128)} async-done(((f32[512,2048]{1,0:T(8,128)}), f32[512,2048]{1,0:T(8,128)}) %all-reduce.12.cloned.1.call-update) | async-done | bytes 4194320 | tf_op jit(solution)/shard_map/psum | solution.py:163
  271.9 48.9 %all-reduce.10.cloned.1.call-done = bf16[512,2048]{1,0:T(8,128)(2,1)} async-done(((bf16[512,2048]{1,0:T(8,128)(2,1)}), bf16[512,2048]{1,0:T(8,128)(2,1)}) %all-reduce.10.cloned.1.call-update) | async-done | bytes 2097168 | tf_op jit(solution)/shard_map/psum | solution.py:151
  320.7 7.0 multiply_add_fusion
  329.7 9.2 while.62
  339.6 18.1 %while.63 = (s32[]{:T(128)}, f32[512,1,8,64]{0,3,2,1:T(8,128)S(1)}, f32[1024,128]{0,1:T(8,128)S(1)}, bf16[1024,128]{0,1:T(8,128)(2,1)S(1)}, s32[512]{0:T(512)S(1...) while((s32[]{:T(128)}, f32[512,1,8,64]{0,3,2,1:T(8,128)S(1)}, ...), condition=%wide.region_16.17_spmd.clone, body=%wide.region_15.16_spmd.clone.sunk | while | flops 1364886528 | bytes 44171576 | solution.py:228
  363.6 9.8 reduce-scatter.9.cloned.1.call-done
  395.4 6.2 fusion.110
  419.2 45.6 %all-reduce.14.cloned.1.call-done = f32[512,2048]{1,0:T(8,128)} async-done(((f32[512,2048]{1,0:T(8,128)}), f32[512,2048]{1,0:T(8,128)}) %all-reduce.14.cloned.1.call-update) | async-done | bytes 4194320 | tf_op jit(solution)/shard_map/psum | solution.py:244
  468.1 37.2 %all-reduce.2 = (f32[2048]{0:T(1024)S(1)}, f32[2048]{0:T(1024)S(1)}) all-reduce(f32[2048]{0:T(1024)S(1)} %get-tuple-element.837, f32[2048]{0:T(1024)S(1)} %copy-done.39), channel_id=3, replica_groups=mesh['dp'=4,'ctx'=2,'tp'=4] {'dp','ctx'}, use_global_device_ids=true, to_apply=%region_21.22.clone | all-reduce | flops 4096 | bytes 32768
  506.6 7.3 fusion.82
  513.9 17.9 %reduce-scatter.13.cloned.1.call-done = f32[256,64]{0,1:T(8,128)} async-done(((f32[2048,64]{0,1:T(8,128)}), f32[256,64]{0,1:T(8,128)}) %reduce-scatter.13.cloned.1.call-update) | async-done | bytes 65552 | tf_op jit(solution)/shard_map/reduce_scatter | solution.py:255
  531.8 66.0 %reduce-scatter.15.cloned.1.call-done = f32[256,64]{0,1:T(8,128)} async-done(((f32[2048,64]{0,1:T(8,128)}), f32[256,64]{0,1:T(8,128)}) %reduce-scatter.15.cloned.1.call-update) | async-done | bytes 65552 | tf_op jit(solution)/shard_map/reduce_scatter | solution.py:256
  597.8 91.6 %reduce-scatter.11.cloned.1.call-done = f32[256,512]{1,0:T(8,128)} async-done(((f32[2048,512]{1,0:T(8,128)}), f32[256,512]{1,0:T(8,128)}) %reduce-scatter.11.cloned.1.call-update) | async-done | bytes 524304 | tf_op jit(solution)/shard_map/reduce_scatter | solution.py:254
  689.4 92.6 %reduce-scatter.17.cloned.1.call-done = f32[512,256]{1,0:T(8,128)} async-done(((f32[512,2048]{1,0:T(8,128)}), f32[512,256]{1,0:T(8,128)}) %reduce-scatter.17.cloned.1.call-update) | async-done | bytes 524304 | tf_op jit(solution)/shard_map/reduce_scatter | solution.py:257
  781.9 196.4 %reduce-scatter.21.cloned.1.call-done = f32[256,1408]{1,0:T(8,128)} async-done(((f32[2048,1408]{1,0:T(8,128)}), f32[256,1408]{1,0:T(8,128)}) %reduce-scatter.21.cloned.1.call-update) | async-done | bytes 1441808 | tf_op jit(solution)/shard_map/reduce_scatter | solution.py:260
  978.4 196.1 %reduce-scatter.19.cloned.1.call-done = f32[256,1408]{1,0:T(8,128)} async-done(((f32[2048,1408]{1,0:T(8,128)}), f32[256,1408]{1,0:T(8,128)}) %reduce-scatter.19.cloned.1.call-update) | async-done | bytes 1441808 | tf_op jit(solution)/shard_map/reduce_scatter | solution.py:259
  1174.4 196.4 %reduce-scatter.23.cloned.1.call-done = f32[1408,256]{1,0:T(8,128)} async-done(((f32[1408,2048]{1,0:T(8,128)}), f32[1408,256]{1,0:T(8,128)}) %reduce-scatter.23.cloned.1.call-update) | async-done | bytes 1441808 | tf_op jit(solution)/shard_map/reduce_scatter | solution.py:261
  (253 shorter events, 145.5 us)
Async XLA Ops:
  7.2 46.3 %copy-start = (bf16[512,2048]{1,0:T(8,128)(2,1)S(1)}, bf16[512,2048]{1,0:T(8,128)(2,1)}, u32[]{:S(2)}) copy-start(bf16[512,2048]{1,0:T(8,128)(2,1)} %param.26) | copy-start | bytes 6291460
  7.2 136.7 %all-reduce.8.cloned.1.call-start = ((), (), s32[]{:S(2)}) async-start(), calls=%async_computation.8 | async-start | bytes 8388608 | tf_op jit(solution)/shard_map/psum | solution.py:143
  56.8 90.7 %copy-start.38 = (f32[2048]{0:T(1024)S(1)}, f32[2048]{0:T(1024)}, u32[]{:S(2)}) copy-start(f32[2048]{0:T(1024)} %param.27) | copy-start | bytes 24580
  56.8 210.0 %all-reduce.12.cloned.1.call-start = ((), (), s32[]{:S(2)}) async-start(), calls=%async_computation.10 | async-start | bytes 8388608 | tf_op jit(solution)/shard_map/psum | solution.py:163
  147.4 15.6 %slice-start.4 = ((s8[5767168]{0:T(1024)(128)(4,1)}), s8[4194304]{0:T(1024)(128)(4,1)S(1)}, s32[]{:S(2)}) async-start(s8[5767168]{0:T(1024)(128)(4,1)} %bitcast.337), calls=%async_computation.24 | async-start | bytes 8388608
  147.9 15.1 %slice-start.5 = ((s8[5767168]{0:T(1024)(128)(4,1)}), s8[1572864]{0:T(1024)(128)(4,1)S(1)}, s32[]{:S(2)}) async-start(s8[5767168]{0:T(1024)(128)(4,1)} %bitcast.337), calls=%async_computation.25 | async-start | bytes 3145728
  158.0 18.0 %slice-start.2 = ((s8[5767168]{0:T(1024)(128)(4,1)}), s8[4194304]{0:T(1024)(128)(4,1)S(1)}, s32[]{:S(2)}) async-start(s8[5767168]{0:T(1024)(128)(4,1)} %bitcast.335), calls=%async_computation.22 | async-start | bytes 8388608
  181.0 139.7 %all-reduce.10.cloned.1.call-start = ((), (), s32[]{:S(2)}) async-start(), calls=%async_computation.9 | async-start | bytes 4194304 | tf_op jit(solution)/shard_map/psum | solution.py:151
  188.9 184.4 %reduce-scatter.9.cloned.1.call-start = ((), (), s32[]{:S(2)}) async-start(), calls=%async_computation.11 | async-start | bytes 786432 | tf_op jit(solution)/shard_map/reduce_scatter | solution.py:229
  339.6 19.2 %copy-start.20 = (f32[512,64]{0,1:T(8,128)S(1)}, f32[512,64]{0,1:T(8,128)}, u32[]{:S(2)}) copy-start(f32[512,64]{0,1:T(8,128)} %copy-done.19) | copy-start | bytes 393220
  358.5 106.3 %all-reduce.14.cloned.1.call-start = ((), (), s32[]{:S(2)}) async-start(), calls=%async_computation.12 | async-start | bytes 8388608 | tf_op jit(solution)/shard_map/psum | solution.py:244
  360.3 15.4 %copy-start.24 = (bf16[2048,64]{0,1:T(8,128)(2,1)S(1)}, bf16[2048,64]{0,1:T(8,128)(2,1)}, u32[]{:S(2)}) copy-start(bf16[2048,64]{0,1:T(8,128)(2,1)} %param.24) | copy-start | bytes 786436
  379.1 152.6 %reduce-scatter.13.cloned.1.call-start = ((), (), s32[]{:S(2)}) async-start(), calls=%async_computation.14 | async-start | bytes 589824 | tf_op jit(solution)/shard_map/reduce_scatter | solution.py:255
  382.0 215.8 %reduce-scatter.15.cloned.1.call-start = ((), (), s32[]{:S(2)}) async-start(), calls=%async_computation.15 | async-start | bytes 589824 | tf_op jit(solution)/shard_map/reduce_scatter | solution.py:256
  383.4 306.0 %reduce-scatter.11.cloned.1.call-start = ((), (), s32[]{:S(2)}) async-start(), calls=%async_computation.13 | async-start | bytes 4718592 | tf_op jit(solution)/shard_map/reduce_scatter | solution.py:254
  386.7 395.2 %reduce-scatter.17.cloned.1.call-start = ((), (), s32[]{:S(2)}) async-start(), calls=%async_computation.16 | async-start | bytes 4718592 | tf_op jit(solution)/shard_map/reduce_scatter | solution.py:257
  393.3 585.0 %reduce-scatter.21.cloned.1.call-start = ((), (), s32[]{:S(2)}) async-start(), calls=%async_computation.18 | async-start | bytes 12976128 | tf_op jit(solution)/shard_map/reduce_scatter | solution.py:260
  401.6 772.8 %reduce-scatter.19.cloned.1.call-start = ((), (), s32[]{:S(2)}) async-start(), calls=%async_computation.17 | async-start | bytes 12976128 | tf_op jit(solution)/shard_map/reduce_scatter | solution.py:259
  409.3 961.5 %reduce-scatter.23.cloned.1.call-start = ((), (), s32[]{:S(2)}) async-start(), calls=%async_computation.19 | async-start | bytes 12976128 | tf_op jit(solution)/shard_map/reduce_scatter | solution.py:261
  417.3 47.5 %copy-start.5 = (bf16[512,2048]{1,0:T(8,128)(2,1)S(1)}, bf16[512,2048]{1,0:T(8,128)(2,1)}, u32[]{:S(2)}) copy-start(bf16[512,2048]{1,0:T(8,128)(2,1)} %param.20) | copy-start | bytes 6291460
  417.3 47.5 %copy-start.37 = (f32[2048]{0:T(1024)S(1)}, f32[2048]{0:T(1024)}, u32[]{:S(2)}) copy-start(f32[2048]{0:T(1024)} %param.22) | copy-start | bytes 24580
  417.3 47.5 %copy-start.41 = (f32[512]{0:T(512)S(1)}, f32[512]{0:T(512)}, u32[]{:S(2)}) copy-start(f32[512]{0:T(512)} %copy-done.40) | copy-start | bytes 6148
  417.4 50.7 %copy-start.39 = (f32[2048]{0:T(1024)S(1)}, f32[2048]{0:T(1024)}, u32[]{:S(2)}) copy-start(f32[2048]{0:T(1024)} %get-tuple-element.835) | copy-start | bytes 24580
  506.6 864.2 %copy-start.1 = (bf16[512,2048]{1,0:T(8,128)(2,1)S(1)}, bf16[512,2048]{1,0:T(8,128)(2,1)}, u32[]{:S(2)}) copy-start(bf16[512,2048]{1,0:T(8,128)(2,1)} %param.26) | copy-start | bytes 6291460
  (47 other events, 205.9 us)
Sparse Core Ops, SparseCore 0:
  56.9 86.9 all-reduce.7
  181.2 85.5 all-reduce.11
  269.2 51.5 all-reduce.9
  358.6 14.6 reduce-scatter.8
  379.3 85.4 all-reduce.13
  468.6 63.1 reduce-scatter.12
  535.7 62.0 reduce-scatter.14
  602.0 87.3 reduce-scatter.10
  693.6 88.3 reduce-scatter.16
  785.9 192.3 reduce-scatter.20
  982.5 191.8 reduce-scatter.18
  1178.4 192.3 reduce-scatter.22
where the time goes:
time: 1380 us
  waiting for transfers between devices  1130 us (82%)
  matrix products  122 us (9%)
  other arithmetic  48.4 us (4%)
  blocking collectives  44.5 us (3%)
  local copies, waits for them, and re-layouts  19.5 us (1%)
  between operations  15.7 us (1%)
    reduce_scatter x1, waiting for transfers between devices, shards(): lax.psum_scatter(mlp_done[1], ('dp', 'ctx'), scatter_dimension=0, tiled=T...  196 us
    reduce_scatter x1, waiting for transfers between devices, shards(): lax.psum_scatter(mlp_done[2], ('dp', 'ctx'), scatter_dimension=1, tiled=T...  196 us
    reduce_scatter x1, waiting for transfers between devices, shards(): lax.psum_scatter(mlp_done[0], ('dp', 'ctx'), scatter_dimension=0, tiled=T...  196 us
    reduce_scatter x1, waiting for transfers between devices, shards(): lax.psum_scatter(output_grad, ('dp', 'ctx'), scatter_dimension=1, tiled=T...  92.6 us
    reduce_scatter x1, waiting for transfers between devices, shards(): lax.psum_scatter(query_grad, ('dp', 'ctx'), scatter_dimension=0, tiled=True)  91.6 us
    psum x1, waiting for transfers between devices, shards(): branch = lax.psum(contract(heads_out, output_weight, 1, 0), 'tp')  86.9 us
    dot_general x21, matrix products, contract(): lax.dot_general(left_side, right_side, (((left_dim,), (right_dim,)), ((),...  84.8 us
    psum x1, waiting for transfers between devices, shards(): lax.psum(contract(gate_back, gate_weight, 1, 1) + contract(up_back, up_we...  77.4 us
  transfers between devices with their start and end apart: 12, of which 12 were waited for; matrix products, arithmetic and copies ran while one was open for 4% of the time, Pallas kernels for 0%

commit v1 on v0

--- a/solution.py
+++ b/solution.py
@@ -140,7 +140,8 @@
         0, ctx_count, out_step, jnp.zeros((row_count, kv_local, groups, HEAD), jnp.float32)
     )
     heads_out = mixed_heads.reshape(row_count, q_local * HEAD).astype(jnp.bfloat16)
-    branch = lax.psum(contract(heads_out, output_weight, 1, 0), "tp")
+    packet = contract(heads_out, output_weight, 1, 0)
+    branch = jnp.sum(lax.all_gather(packet, "tp"), 0)
     middle = tokens_wide + branch
     normed_two, inverse_two, mlp_in = rms_parts(middle, mlp_gain)
     gate_pre = contract(mlp_in, gate_weight, 1, 0)

time: 1380 us -> 1410 us (1.022)
    all_gather x0 -> x1, waiting for transfers between devices: none -> 107 us  [shards(): branch = jnp.sum(lax.all_gather(packet, 'tp'), 0)]
    psum x1 -> x0, waiting for transfers between devices: 86.9 us -> none  [shards(): branch = lax.psum(contract(heads_out, output_weight, 1, 0), 'tp')]
where the time goes in v1:
time: 1410 us
  waiting for transfers between devices  1140 us (81%)
  matrix products  126 us (9%)
  other arithmetic  58.5 us (4%)
  blocking collectives  44.5 us (3%)
  local copies, waits for them, and re-layouts  17.9 us (1%)
  between operations  15.7 us (1%)
    reduce_scatter x1, waiting for transfers between devices, shards(): lax.psum_scatter(mlp_done[1], ('dp', 'ctx'), scatter_dimension=0, tiled=T...  196 us
    reduce_scatter x1, waiting for transfers between devices, shards(): lax.psum_scatter(mlp_done[2], ('dp', 'ctx'), scatter_dimension=1, tiled=T...  196 us
    reduce_scatter x1, waiting for transfers between devices, shards(): lax.psum_scatter(mlp_done[0], ('dp', 'ctx'), scatter_dimension=0, tiled=T...  196 us
    all_gather x1, waiting for transfers between devices, shards(): branch = jnp.sum(lax.all_gather(packet, 'tp'), 0)  107 us
    reduce_scatter x1, waiting for transfers between devices, shards(): lax.psum_scatter(output_grad, ('dp', 'ctx'), scatter_dimension=1, tiled=T...  92.6 us
    reduce_scatter x1, waiting for transfers between devices, shards(): lax.psum_scatter(query_grad, ('dp', 'ctx'), scatter_dimension=0, tiled=True)  91.6 us
    dot_general x21, matrix products, contract(): lax.dot_general(left_side, right_side, (((left_dim,), (right_dim,)), ((),...  89.1 us
    psum x1, waiting for transfers between devices, shards(): lax.psum(contract(gate_back, gate_weight, 1, 1) + contract(up_back, up_we...  77.7 us
  transfers between devices with their start and end apart: 12, of which 12 were waited for; matrix products, arithmetic and copies ran while one was open for 4% of the time, Pallas kernels for 0%

profile of v1, /device:TPU:0, one launch (start us, length us, event | category | flops | bytes accessed | tf_op | source)
XLA Modules:
  0.0 1409.2 jit_solution(8397396174476878567)
XLA Ops:
  27.1 11.2 while.60
  39.0 12.4 while.61
  57.1 107.3 %all-gather.3.cloned.1.call-done = f32[2048,2048]{1,0:T(8,128)} async-done(((f32[512,2048]{1,0:T(8,128)}), f32[2048,2048]{1,0:T(8,128)}) %all-gather.3.cloned.1.call-update) | async-done | bytes 16777232 | tf_op jit(solution)/shard_map/all_gather | solution.py:144
  164.4 10.2 reduce_sum.90
  178.6 10.0 fusion.104
  193.7 8.3 multiply_convert_fusion.1
  212.0 7.8 convolution_convert_fusion
  219.9 77.7 %all-reduce.9.cloned.1.call-done = f32[512,2048]{1,0:T(8,128)} async-done(((f32[512,2048]{1,0:T(8,128)}), f32[512,2048]{1,0:T(8,128)}) %all-reduce.9.cloned.1.call-update) | async-done | bytes 4194320 | tf_op jit(solution)/shard_map/psum | solution.py:164
  302.7 48.9 %all-reduce.7.cloned.1.call-done = bf16[512,2048]{1,0:T(8,128)(2,1)} async-done(((bf16[512,2048]{1,0:T(8,128)(2,1)}), bf16[512,2048]{1,0:T(8,128)(2,1)}) %all-reduce.7.cloned.1.call-update) | async-done | bytes 2097168 | tf_op jit(solution)/shard_map/psum | solution.py:152
  351.6 7.4 multiply_add_fusion
  361.0 9.2 while.62
  370.8 18.1 %while.63 = (s32[]{:T(128)}, f32[512,1,8,64]{0,3,2,1:T(8,128)S(1)}, f32[1024,128]{0,1:T(8,128)S(1)}, bf16[1024,128]{0,1:T(8,128)(2,1)S(1)}, s32[512]{0:T(512)S(1...) while((s32[]{:T(128)}, f32[512,1,8,64]{0,3,2,1:T(8,128)S(1)}, ...), condition=%wide.region_16.17_spmd.clone, body=%wide.region_15.16_spmd.clone.sunk | while | flops 1364886528 | bytes 44171576 | solution.py:229
  394.9 9.8 reduce-scatter.9.cloned.1.call-done
  426.2 7.6 fusion.110
  433.9 7.6 fusion.109
  452.3 43.8 %all-reduce.11.cloned.1.call-done = f32[512,2048]{1,0:T(8,128)} async-done(((f32[512,2048]{1,0:T(8,128)}), f32[512,2048]{1,0:T(8,128)}) %all-reduce.11.cloned.1.call-update) | async-done | bytes 4194320 | tf_op jit(solution)/shard_map/psum | solution.py:245
  499.4 37.2 %all-reduce.2 = (f32[2048]{0:T(1024)S(1)}, f32[2048]{0:T(1024)S(1)}) all-reduce(f32[2048]{0:T(1024)S(1)} %get-tuple-element.837, f32[2048]{0:T(1024)S(1)} %copy-done.40), channel_id=4, replica_groups=mesh['dp'=4,'ctx'=2,'tp'=4] {'dp','ctx'}, use_global_device_ids=true, to_apply=%region_21.22.clone | all-reduce | flops 4096 | bytes 32768
  545.2 17.9 %reduce-scatter.13.cloned.1.call-done = f32[256,64]{0,1:T(8,128)} async-done(((f32[2048,64]{0,1:T(8,128)}), f32[256,64]{0,1:T(8,128)}) %reduce-scatter.13.cloned.1.call-update) | async-done | bytes 65552 | tf_op jit(solution)/shard_map/reduce_scatter | solution.py:256
  563.1 66.0 %reduce-scatter.15.cloned.1.call-done = f32[256,64]{0,1:T(8,128)} async-done(((f32[2048,64]{0,1:T(8,128)}), f32[256,64]{0,1:T(8,128)}) %reduce-scatter.15.cloned.1.call-update) | async-done | bytes 65552 | tf_op jit(solution)/shard_map/reduce_scatter | solution.py:257
  629.0 91.6 %reduce-scatter.11.cloned.1.call-done = f32[256,512]{1,0:T(8,128)} async-done(((f32[2048,512]{1,0:T(8,128)}), f32[256,512]{1,0:T(8,128)}) %reduce-scatter.11.cloned.1.call-update) | async-done | bytes 524304 | tf_op jit(solution)/shard_map/reduce_scatter | solution.py:255
  720.7 92.6 %reduce-scatter.17.cloned.1.call-done = f32[512,256]{1,0:T(8,128)} async-done(((f32[512,2048]{1,0:T(8,128)}), f32[512,256]{1,0:T(8,128)}) %reduce-scatter.17.cloned.1.call-update) | async-done | bytes 524304 | tf_op jit(solution)/shard_map/reduce_scatter | solution.py:258
  813.2 196.4 %reduce-scatter.21.cloned.1.call-done = f32[256,1408]{1,0:T(8,128)} async-done(((f32[2048,1408]{1,0:T(8,128)}), f32[256,1408]{1,0:T(8,128)}) %reduce-scatter.21.cloned.1.call-update) | async-done | bytes 1441808 | tf_op jit(solution)/shard_map/reduce_scatter | solution.py:261
  1009.7 196.1 %reduce-scatter.19.cloned.1.call-done = f32[256,1408]{1,0:T(8,128)} async-done(((f32[2048,1408]{1,0:T(8,128)}), f32[256,1408]{1,0:T(8,128)}) %reduce-scatter.19.cloned.1.call-update) | async-done | bytes 1441808 | tf_op jit(solution)/shard_map/reduce_scatter | solution.py:260
  1205.7 196.4 %reduce-scatter.23.cloned.1.call-done = f32[1408,256]{1,0:T(8,128)} async-done(((f32[1408,2048]{1,0:T(8,128)}), f32[1408,256]{1,0:T(8,128)}) %reduce-scatter.23.cloned.1.call-update) | async-done | bytes 1441808 | tf_op jit(solution)/shard_map/reduce_scatter | solution.py:262
  (250 shorter events, 152.6 us)
Async XLA Ops:
  7.2 46.3 %copy-start = (bf16[512,2048]{1,0:T(8,128)(2,1)S(1)}, bf16[512,2048]{1,0:T(8,128)(2,1)}, u32[]{:S(2)}) copy-start(bf16[512,2048]{1,0:T(8,128)(2,1)} %param.26) | copy-start | bytes 6291460
  7.2 157.2 %all-gather.3.cloned.1.call-start = ((), (), s32[]{:S(2)}) async-start(), calls=%async_computation.19 | async-start | bytes 20971520 | tf_op jit(solution)/shard_map/all_gather | solution.py:144
  56.8 240.8 %all-reduce.9.cloned.1.call-start = ((), (), s32[]{:S(2)}) async-start(), calls=%async_computation.9 | async-start | bytes 8388608 | tf_op jit(solution)/shard_map/psum | solution.py:164
  178.1 15.6 %slice-start.4 = ((s8[5767168]{0:T(1024)(128)(4,1)}), s8[4194304]{0:T(1024)(128)(4,1)S(1)}, s32[]{:S(2)}) async-start(s8[5767168]{0:T(1024)(128)(4,1)} %bitcast.339), calls=%async_computation.24 | async-start | bytes 8388608
  178.6 15.1 %slice-start.5 = ((s8[5767168]{0:T(1024)(128)(4,1)}), s8[1572864]{0:T(1024)(128)(4,1)S(1)}, s32[]{:S(2)}) async-start(s8[5767168]{0:T(1024)(128)(4,1)} %bitcast.339), calls=%async_computation.25 | async-start | bytes 3145728
  188.6 18.3 %slice-start.2 = ((s8[5767168]{0:T(1024)(128)(4,1)}), s8[4194304]{0:T(1024)(128)(4,1)S(1)}, s32[]{:S(2)}) async-start(s8[5767168]{0:T(1024)(128)(4,1)} %bitcast.337), calls=%async_computation.22 | async-start | bytes 8388608
  212.0 139.6 %all-reduce.7.cloned.1.call-start = ((), (), s32[]{:S(2)}) async-start(), calls=%async_computation.8 | async-start | bytes 4194304 | tf_op jit(solution)/shard_map/psum | solution.py:152
  219.9 184.7 %reduce-scatter.9.cloned.1.call-start = ((), (), s32[]{:S(2)}) async-start(), calls=%async_computation.10 | async-start | bytes 786432 | tf_op jit(solution)/shard_map/reduce_scatter | solution.py:230
  370.8 19.2 %copy-start.20 = (f32[512,64]{0,1:T(8,128)S(1)}, f32[512,64]{0,1:T(8,128)}, u32[]{:S(2)}) copy-start(f32[512,64]{0,1:T(8,128)} %copy-done.19) | copy-start | bytes 393220
  389.8 106.3 %all-reduce.11.cloned.1.call-start = ((), (), s32[]{:S(2)}) async-start(), calls=%async_computation.11 | async-start | bytes 8388608 | tf_op jit(solution)/shard_map/psum | solution.py:245
  391.6 14.1 %copy-start.33 = (f32[512,32]{0,1:T(8,128)S(1)}, f32[512,32]{0,1:T(8,128)}, u32[]{:S(2)}) copy-start(f32[512,32]{0,1:T(8,128)} %copy-done.32) | copy-start | bytes 196612
  391.6 15.4 %copy-start.24 = (bf16[2048,64]{0,1:T(8,128)(2,1)S(1)}, bf16[2048,64]{0,1:T(8,128)(2,1)}, u32[]{:S(2)}) copy-start(bf16[2048,64]{0,1:T(8,128)(2,1)} %param.24) | copy-start | bytes 786436
  410.4 152.6 %reduce-scatter.13.cloned.1.call-start = ((), (), s32[]{:S(2)}) async-start(), calls=%async_computation.13 | async-start | bytes 589824 | tf_op jit(solution)/shard_map/reduce_scatter | solution.py:256
  413.3 215.8 %reduce-scatter.15.cloned.1.call-start = ((), (), s32[]{:S(2)}) async-start(), calls=%async_computation.14 | async-start | bytes 589824 | tf_op jit(solution)/shard_map/reduce_scatter | solution.py:257
  414.6 306.0 %reduce-scatter.11.cloned.1.call-start = ((), (), s32[]{:S(2)}) async-start(), calls=%async_computation.12 | async-start | bytes 4718592 | tf_op jit(solution)/shard_map/reduce_scatter | solution.py:255
  418.0 395.2 %reduce-scatter.17.cloned.1.call-start = ((), (), s32[]{:S(2)}) async-start(), calls=%async_computation.15 | async-start | bytes 4718592 | tf_op jit(solution)/shard_map/reduce_scatter | solution.py:258
  424.6 585.0 %reduce-scatter.21.cloned.1.call-start = ((), (), s32[]{:S(2)}) async-start(), calls=%async_computation.17 | async-start | bytes 12976128 | tf_op jit(solution)/shard_map/reduce_scatter | solution.py:261
  433.8 771.9 %reduce-scatter.19.cloned.1.call-start = ((), (), s32[]{:S(2)}) async-start(), calls=%async_computation.16 | async-start | bytes 12976128 | tf_op jit(solution)/shard_map/reduce_scatter | solution.py:260
  441.5 960.6 %reduce-scatter.23.cloned.1.call-start = ((), (), s32[]{:S(2)}) async-start(), calls=%async_computation.18 | async-start | bytes 12976128 | tf_op jit(solution)/shard_map/reduce_scatter | solution.py:262
  450.4 45.7 %copy-start.5 = (bf16[512,2048]{1,0:T(8,128)(2,1)S(1)}, bf16[512,2048]{1,0:T(8,128)(2,1)}, u32[]{:S(2)}) copy-start(bf16[512,2048]{1,0:T(8,128)(2,1)} %param.20) | copy-start | bytes 6291460
  450.4 45.7 %copy-start.38 = (f32[2048]{0:T(1024)S(1)}, f32[2048]{0:T(1024)}, u32[]{:S(2)}) copy-start(f32[2048]{0:T(1024)} %param.22) | copy-start | bytes 24580
  450.4 45.7 %copy-start.42 = (f32[512]{0:T(512)S(1)}, f32[512]{0:T(512)}, u32[]{:S(2)}) copy-start(f32[512]{0:T(512)} %copy-done.41) | copy-start | bytes 6148
  450.5 48.9 %copy-start.40 = (f32[2048]{0:T(1024)S(1)}, f32[2048]{0:T(1024)}, u32[]{:S(2)}) copy-start(f32[2048]{0:T(1024)} %get-tuple-element.835) | copy-start | bytes 24580
  537.9 864.2 %copy-start.1 = (bf16[512,2048]{1,0:T(8,128)(2,1)S(1)}, bf16[512,2048]{1,0:T(8,128)(2,1)}, u32[]{:S(2)}) copy-start(bf16[512,2048]{1,0:T(8,128)(2,1)} %param.26) | copy-start | bytes 6291460
  (45 other events, 206.9 us)
Sparse Core Ops, SparseCore 0:
  56.9 107.3 all-gather.2
  212.1 85.4 all-reduce.8
  300.0 51.5 all-reduce.6
  389.9 14.6 reduce-scatter.8
  410.5 85.4 all-reduce.10
  499.8 63.1 reduce-scatter.12
  567.0 62.0 reduce-scatter.14
  633.2 87.3 reduce-scatter.10
  724.9 88.3 reduce-scatter.16
  817.2 192.3 reduce-scatter.20
  1013.8 191.8 reduce-scatter.18
  1209.7 192.3 reduce-scatter.22
